TPU v7x, 256 devices: a whole 4x4x8 slice. The times are simulated.
256 devices in a mesh: rep: 4 (over z_hi), own: 64 (over x, z_lo, y, core).
Axes of the slice: x: 4, y: 4, z: 8 (z_hi: 4, z_lo: 2; z = z_hi * 2 + z_lo), core: 2. Of those that a mesh axis runs over, the one named last changes fastest.
Arguments:
- inputs: bfloat16 [65536, 8192], P(('rep', 'own')), may hold values from -24 to 24
- cotangent: bfloat16 [65536, 8192], P(('rep', 'own')), may hold values from -6 to 6
- gate: float32 [65536], P(('rep', 'own')), may hold values from 0.05 to 0.95
- down_weight: bfloat16 [8192, 256], P('rep'), may hold values from -0.0625 to 0.0625
- up_weight: bfloat16 [8192, 256], P('rep'), may hold values from -0.0625 to 0.0625
- mixing: bfloat16 [256, 256], replicated, may hold values from -0.375 to 0.375
- owner_table: int32 [64, 1], replicated, may hold values from -1 to 31, as said below
- left_factor: float32 [64, 256, 256], P('own'), as said below
- right_factor: float32 [64, 256, 256], P('own'), as said below
Outputs:
- preconditioned: float32 [16384, 256], P('own')
Inputs may be any that keep to these rules, and one draw needn't show every extreme that they name: `owner_table`: each of the 32 block ids stands in exactly one slot; -1 marks an empty slot; some owner has all 1 slots filled. `left_factor`: every slot's matrix is symmetric positive definite. `right_factor`: every slot's matrix is symmetric positive definite.
All inputs are finite; a program needn't handle non-finite values.
Results may differ from a plain program's by a relative error of at most 0.0077.
Values may be sent and summed in bfloat16 or wider, within the bound.
A program may use at most 128 MiB of HBM per device.

v0:
```python
import jax
import jax.numpy as jnp
from jax import lax
from jax.sharding import PartitionSpec as P

R = 256
ITERS = 5


BETA = 0.95
EPS = 1e-06


def in_blocks(shard, dim, size):
    before, after = (shard.shape[:dim], shard.shape[dim + 1 :])
    return jnp.moveaxis(shard.reshape(*before, size, -1, *after), dim, 0)


def sent_and_summed(shard, axis, dim):
    parts = in_blocks(shard, dim, lax.axis_size(axis))
    arrived = lax.all_to_all(parts, axis, split_axis=0, concat_axis=0, tiled=True)
    return arrived.astype(jnp.float32).sum(axis=0)


def from_everyone(shard, axis):
    size = lax.axis_size(axis)
    return lax.all_to_all(
        jnp.broadcast_to(shard[None], (size, *shard.shape)), axis, 0, 0, tiled=True
    )


def over_copies(shard, axis):
    return from_everyone(shard, axis).sum(axis=0)


def batched(left, right):
    return jnp.einsum("kij,kjl->kil", left, right, precision=lax.Precision.HIGHEST)


def inverse_root(matrices):
    width = matrices.shape[-1]
    identity = jnp.eye(width, dtype=jnp.float32)
    shifted = matrices + EPS * identity
    norm_size = jnp.sqrt(jnp.sum(shifted * shifted, axis=(1, 2)))
    result = jnp.broadcast_to(identity, shifted.shape) * (norm_size ** (-0.25))[:, None, None]
    normed = shifted / norm_size[:, None, None]
    for sweep in range(ITERS):
        factor = (5.0 * identity - normed) / 4.0
        result = batched(result, factor)
        square = batched(factor, factor)
        normed = batched(batched(square, square), normed)
    return result


def shards(
    inputs, cotangent, gate, down_weight, up_weight, mixing, owner_table, left_factor, right_factor
):
    token_total = inputs.shape[0] * lax.axis_size("rep") * lax.axis_size("own")
    slot_count = left_factor.shape[0]
    lifted = (gate[:, None] * inputs.astype(jnp.float32) * cotangent.astype(jnp.float32)).astype(
        jnp.bfloat16
    )
    columns = inputs
    projected = jnp.dot(
        columns,
        lax.all_gather(down_weight, "rep", axis=0, tiled=True),
        preferred_element_type=jnp.float32,
    )
    back_proj = jnp.dot(
        lifted,
        lax.all_gather(up_weight, "rep", axis=0, tiled=True),
        preferred_element_type=jnp.float32,
    )
    inner_act = jnp.tanh(projected).astype(jnp.bfloat16)
    outer_act = jnp.tanh(jnp.dot(inner_act, mixing, preferred_element_type=jnp.float32))
    outer_slope = (back_proj * (1.0 - outer_act * outer_act)).astype(jnp.bfloat16)
    through = lax.dot_general(
        outer_slope, mixing, (((1,), (1,)), ((), ())), preferred_element_type=jnp.float32
    )
    inner_wide = inner_act.astype(jnp.float32)
    signal = (through * (1.0 - inner_wide * inner_wide)).astype(jnp.bfloat16)
    columns = inputs
    shard = sent_and_summed(
        (
            lax.dot_general(
                columns, signal, (((0,), (0,)), ((), ())), preferred_element_type=jnp.float32
            )
            / token_total
        ).astype(jnp.bfloat16),
        "own",
        0,
    )
    shard = over_copies(shard, "rep")
    my_blocks = lax.dynamic_index_in_dim(owner_table, lax.axis_index("own"), 0, keepdims=False)
    wanted = (
        jnp.maximum(my_blocks, 0)[:, None] * R + jnp.arange(R, dtype=jnp.int32)[None, :]
    ).reshape(-1)
    shard_rows = lax.all_gather(shard, "own", axis=0, tiled=True)
    row_total = shard_rows.shape[0]
    inside = (wanted >= 0) & (wanted < row_total)
    selected = jnp.take(shard_rows, jnp.clip(wanted, 0, row_total - 1), axis=0)
    owned = jnp.where(inside[:, None], selected, jnp.zeros((slot_count * R, R), jnp.float32))
    my_row = lax.dynamic_index_in_dim(owner_table, lax.axis_index("own"), 0, keepdims=False)
    filled_slots = (my_row >= 0)[:, None, None]
    gradients = jnp.where(filled_slots, owned.reshape(slot_count, R, R), 0.0)
    flipped = jnp.swapaxes(gradients, 1, 2)
    left_new = BETA * left_factor + (1.0 - BETA) * batched(gradients, flipped)
    right_new = BETA * right_factor + (1.0 - BETA) * batched(flipped, gradients)
    factors = jnp.concatenate([left_new, right_new], axis=0)
    inverse_roots = inverse_root(factors)
    preconditioned = batched(
        batched(inverse_roots[:slot_count], gradients), inverse_roots[slot_count:]
    )
    return jnp.where(filled_slots, preconditioned, 0.0).reshape(slot_count * R, R)


def solution(mesh):
    in_specs = (
        P(("rep", "own"), None),
        P(("rep", "own"), None),
        P(("rep", "own")),
        P("rep", None),
        P("rep", None),
        P(),
        P(),
        P("own", None, None),
        P("own", None, None),
    )
    out_specs = P("own", None)
    return jax.shard_map(shards, mesh=mesh, in_specs=in_specs, out_specs=out_specs, check_vma=False)
```

profile of v0, /device:TPU:1, one launch (start us, length us, event | category | flops | bytes accessed | tf_op | source)
XLA Modules:
  0.0 412.4 jit_solution(15941747103290390603)
XLA Ops:
  6.5 0.0 copy-start
  6.5 0.0 all-gather.6.cloned.1.call-start
  6.5 0.7 all-gather.6.cloned.1.call-update
  7.3 0.0 all-gather.4.cloned.1.call-start
  7.3 0.7 all-gather.4.cloned.1.call-update
  8.0 0.0 copy-start.4
  8.0 0.0 all-gather.8.cloned.1.call-start
  8.1 80.3 %all-gather.6.cloned.1.call-done = bf16[8192,256]{1,0:T(8,128)(2,1)} async-done(((bf16[2048,256]{1,0:T(8,128)(2,1)}), bf16[8192,256]{1,0:T(8,128)(2,1)}) %all-gather.6.cloned.1.call-update) | async-done | bytes 4194320 | tf_op jit(solution)/shard_map/all_gather | solution.py:66
  88.3 4.7 %fusion.14 = bf16[256,256]{1,0:T(8,128)(2,1)S(1)} fusion(bf16[256,8192]{1,0:T(8,128)(2,1)} %param.9, bf16[8192,256]{1,0:T(8,128)(2,1)} %all-gather.6.cloned.1.call-done), kind=kOutput, calls=%fused_computation.26 | convolution fusion | flops 1073807360 | bytes 8519680 | tf_op jit(solution)/shard_map/dot_general | solution.py:64
  93.0 81.9 %all-gather.4.cloned.1.call-done = bf16[8192,256]{1,0:T(8,128)(2,1)} async-done(((bf16[2048,256]{1,0:T(8,128)(2,1)}), bf16[8192,256]{1,0:T(8,128)(2,1)}) %all-gather.4.cloned.1.call-update) | async-done | bytes 4194320 | tf_op jit(solution)/shard_map/all_gather | solution.py:71
  175.0 6.1 %fusion.1 = f32[256,256]{1,0:T(8,128)S(1)} fusion(bf16[8192,256]{1,0:T(8,128)(2,1)} %all-gather.4.cloned.1.call-done, bf16[256,8192]{1,0:T(8,128)(2,1)} %param.10, bf16[256,8192]{1,0:T(8,128)(2,1)} %param.9, f32[256]{0:T(256)S(1)} %copy-done.4), kind=kOutput, calls=%fused_computation.5 | convolution fusion | flops 1084227584 | bytes 12846080 | tf_op jit(solution)/shard_map/dot_general | solution.py:69
  181.1 0.0 copy-done
  181.1 0.3 fusion.13
  181.5 3.5 fusion.3
  184.9 1.2 copy.19
  186.1 71.1 %all_to_all.10 = bf16[64,128,256]{1,2,0:T(8,128)(2,1)S(1)} all-to-all(bf16[64,128,256]{1,2,0:T(8,128)(2,1)S(1)} %bitcast.74), channel_id=1, replica_groups=mesh['rep'=4,'own'=64] {'own'}, dimensions={0} | all-to-all | bytes 8388608 | tf_op jit(solution)/shard_map/all_to_all | solution.py:21
  257.2 0.6 convert_reduce_fusion
  257.8 0.0 copy-start.2
  257.9 0.1 copy.15
  258.0 18.4 %all_to_all.11 = f32[4,128,256]{2,1,0:T(8,128)S(1)} all-to-all(f32[4,128,256]{2,1,0:T(8,128)S(1)} %broadcast_in_dim.67), channel_id=1, replica_groups=mesh['rep'=4,'own'=64] {'rep'}, dimensions={0} | all-to-all | bytes 1048576 | tf_op jit(solution)/shard_map/all_to_all | solution.py:27
  276.4 0.7 reduce_sum.28
  277.1 0.0 all-gather.8.cloned.1.call-update
  277.1 0.7 fusion.91
  279.2 107.1 %all-gather.8.cloned.1.call-done = f32[8192,256]{1,0:T(8,128)} async-done(((f32[128,256]{1,0:T(8,128)}), f32[8192,256]{1,0:T(8,128)}) %all-gather.8.cloned.1.call-update) | async-done | bytes 8388624 | tf_op jit(solution)/shard_map/all_gather | solution.py:98
  386.3 4.3 %gather_fusion = f32[256,256]{1,0:T(8,128)S(1)} fusion(f32[8192,256]{1,0:T(8,128)} %all-gather.8.cloned.1.call-done, s32[1024]{0:T(1024)S(1)} %pad_clamp_fusion), kind=kCustom, calls=%fused_computation | custom fusion | bytes 525312 | tf_op jit(solution)/shard_map/jit(_take)/gather | solution.py:101
  390.6 0.0 copy-done.1
  390.6 0.5 fusion.10
  391.2 0.8 fusion.11
  391.9 0.2 multiply_reduce_fusion
  392.2 0.9 fusion.17
  393.0 0.6 fusion.92
  393.7 0.7 fusion.87
  394.5 0.7 fusion.18
  395.2 0.6 fusion.93
  395.9 0.7 fusion.94
  396.5 0.7 fusion.20
  397.3 0.6 fusion.95
  397.9 0.7 fusion.96
  398.6 0.7 fusion.22
  399.3 0.6 fusion.97
  400.0 0.7 fusion.4
  400.7 0.8 fusion.15
  401.5 0.7 fusion.19
  402.2 0.7 fusion.21
  402.9 0.7 fusion.23
  403.6 0.7 fusion.98
  404.3 0.5 fusion.25
  404.7 1.1 convolution_select_fusion
  (12 shorter events, 0.1 us)
Async XLA Ops:
  6.5 174.6 %copy-start = (bf16[256,256]{1,0:T(8,128)(2,1)S(1)}, bf16[256,256]{1,0:T(8,128)(2,1)}, u32[]{:S(2)}) copy-start(bf16[256,256]{1,0:T(8,128)(2,1)} %param.14) | copy-start | bytes 393220
  6.5 81.8 %all-gather.6.cloned.1.call-start = ((), (), s32[]{:S(2)}) async-start(), calls=%async_computation.3 | async-start | bytes 5242880 | tf_op jit(solution)/shard_map/all_gather | solution.py:66
  7.3 167.7 %all-gather.4.cloned.1.call-start = ((), (), s32[]{:S(2)}) async-start(), calls=%async_computation.2 | async-start | bytes 5242880 | tf_op jit(solution)/shard_map/all_gather | solution.py:71
  8.0 167.0 %copy-start.4 = (f32[256]{0:T(256)S(1)}, f32[256]{0:T(256)}, u32[]{:S(2)}) copy-start(f32[256]{0:T(256)} %param.11) | copy-start | bytes 3076
  8.0 378.3 %all-gather.8.cloned.1.call-start = ((), (), s32[]{:S(2)}) async-start(), calls=%async_computation.4 | async-start | bytes 8519680 | tf_op jit(solution)/shard_map/all_gather | solution.py:98
  257.2 19.9 %copy-start.3 = (s32[64,1]{0,1:T(1,128)S(1)}, s32[64,1]{0,1:T(1,128)}, u32[]{:S(2)}) copy-start(s32[64,1]{0,1:T(1,128)} %param.15) | copy-start | bytes 772
  257.2 133.4 %copy-start.1 = (f32[1,256,256]{2,1,0:T(8,128)S(1)}, f32[1,256,256]{2,1,0:T(8,128)}, u32[]{:S(2)}) copy-start(f32[1,256,256]{2,1,0:T(8,128)} %param.16) | copy-start | bytes 786436
  257.8 133.3 %copy-start.2 = (f32[1,256,256]{2,1,0:T(8,128)S(1)}, f32[1,256,256]{2,1,0:T(8,128)}, u32[]{:S(2)}) copy-start(f32[1,256,256]{2,1,0:T(8,128)} %param.17) | copy-start | bytes 786436
Sparse Core Ops, SparseCore 0:
  9.1 79.1 all-gather.5
  90.1 84.8 all-gather.3
  277.2 108.9 all-gather.7
where the time goes:
time: 413 us; the launch traced here: 412 us
  waiting for transfers between devices  271 us (66%)
  blocking collectives  89.5 us (22%)
  matrix products  29.4 us (7%)
  between operations  14.7 us (4%)
  local copies, waits for them, and re-layouts  5.69 us (1%)
    all_gather x1, waiting for transfers between devices, shards(): shard_rows = lax.all_gather(shard, 'own', axis=0, tiled=True)  107 us
    all_gather x1, waiting for transfers between devices, shards(): lax.all_gather(up_weight, 'rep', axis=0, tiled=True)  81.9 us
    all_gather x1, waiting for transfers between devices, shards(): lax.all_gather(down_weight, 'rep', axis=0, tiled=True)  80.3 us
    all_to_all x1, blocking collectives, sent_and_summed(): lax.all_to_all(parts, axis, split_axis=0, concat_axis=0, tiled=True)  71.1 us
    all_to_all x1, blocking collectives, from_everyone(): lax.all_to_all(jnp.broadcast_to(shard[None], (size, *shard.shape)), axis,...  18.4 us
    dot_general x21, matrix products, batched(): jnp.einsum('kij,kjl->kil', left, right, precision=lax.Precision.HIGHEST)  14.8 us
  transfers between devices with their start and end apart: 3, of which 3 were waited for; matrix products, arithmetic and copies ran while one was open for 1% of the time, Pallas kernels for 0%

commit v1 on v0

v1 whole, which is shorter than its diff:
```python
import functools

import jax
import jax.numpy as jnp
from jax import lax
from jax.experimental import pallas as pl
from jax.experimental.pallas import tpu as pltpu
from jax.sharding import PartitionSpec as P

R = 256
ITERS = 5
BETA = 0.95
EPS = 1e-06
TOKENS = 65536

F32 = jnp.float32
BF16 = jnp.bfloat16
MESH = pl.DeviceIdType.MESH


def own_of(x, zl, y, c):
    return ((x * 2 + zl) * 4 + y) * 2 + c


def reduce_kernel(
    x_hbm, cot_hbm, gate_ref, down_hbm, up_hbm, mix_ref, table_ref, out_ref,
    wbuf, xv, lv, gcol, pacc, sigp, dsend, drecv, acc,
    s1send, s1rel, s1recv, s2f, s2send, s2recv, zf, zsend, zrecv, zag, stage, arecv,
    ld, wsend, w1r, st1r, st2r, ddr, gsend, gdr, s1relr, s1r, s2r, zr, zagr, asend, ar,
):
    r = lax.axis_index("rep")
    o = lax.axis_index("own")
    c = lax.rem(o, 2)
    y = lax.rem(o // 2, 4)
    zl = lax.rem(o // 8, 2)
    x = o // 16
    z = r * 2 + zl
    m = (x * 4 + y) * 2 + c
    sgn = 2 * zl - 1
    partner = (r, own_of(x, zl, y, 1 - c))

    def along(axis, d):
        if axis == 0:
            return (r, own_of(lax.rem(x + d + 4, 4), zl, y, c))
        return (r, own_of(x, zl, lax.rem(y + d + 4, 4), c))

    def zpeer(d):
        zz = lax.rem(z + d + 8, 8)
        return (zz // 2, own_of(x, lax.rem(zz, 2), y, c))

    def plane(mm):
        return (r, own_of(mm // 8, zl, lax.rem(mm // 2, 4), lax.rem(mm, 2)))

    quarter = [r, lax.rem(r + sgn + 4, 4), lax.rem(r - sgn + 4, 4), lax.rem(r + 2, 4)]

    pending = []

    def send(src, dst, ssem, rsem, dev):
        cp = pltpu.make_async_remote_copy(
            src_ref=src, dst_ref=dst, send_sem=ssem, recv_sem=rsem,
            device_id=dev, device_id_type=MESH,
        )
        cp.start()
        pending.append(cp)

    def arrived(dst, rsem, dev):
        pltpu.make_async_remote_copy(
            src_ref=dst, dst_ref=dst, send_sem=rsem, recv_sem=rsem,
            device_id=dev, device_id_type=MESH,
        ).wait_recv()

    loads = [
        pltpu.make_async_copy(down_hbm, wbuf.at[0, 0], ld.at[0]),
        pltpu.make_async_copy(up_hbm, wbuf.at[0, 1], ld.at[1]),
    ]
    for s in range(4):
        cols = pl.ds(pl.multiple_of(quarter[s] * 2048, 2048), 2048)
        loads.append(pltpu.make_async_copy(x_hbm.at[:, cols], xv.at[:, cols], ld.at[2 + 2 * s]))
        loads.append(pltpu.make_async_copy(cot_hbm.at[:, cols], lv.at[:, cols], ld.at[3 + 2 * s]))
    for cp in loads:
        cp.start()

    barrier = pltpu.get_barrier_semaphore()

    def greet_z(d, carry):
        pl.semaphore_signal(barrier, inc=1, device_id=zpeer(d), device_id_type=MESH)
        return carry

    def greet_p(e, carry):
        pl.semaphore_signal(
            barrier, inc=1, device_id=plane(lax.rem(m + e, 32)), device_id_type=MESH
        )
        return carry

    lax.fori_loop(1, 8, greet_z, 0)
    lax.fori_loop(1, 32, greet_p, 0)
    pl.semaphore_wait(barrier, 38)

    pos = (x, y)
    nws = [0]

    def wsem():
        nws[0] += 1
        return wsend.at[nws[0] - 1]

    def base(cc, k):
        return cc * 1024 + k * 512

    def piece(slot, k, p1, p2):
        rows = pl.ds(pl.multiple_of(base(c, k) + (p2 * 4 + p1) * 32, 32), 32)
        return rows

    def group(slot, k, p2):
        return pl.ds(pl.multiple_of(base(c, k) + p2 * 128, 128), 128)

    def p12(k):
        return (pos[0], pos[1]) if k == 0 else (pos[1], pos[0])

    def near(p, d):
        return lax.rem(p + d + 4, 4)

    loads[0].wait()
    loads[1].wait()
    zdest = [
        (lax.rem(r + sgn + 4, 4), own_of(x, 1 - zl, y, c)),
        (lax.rem(r + sgn + 4, 4), own_of(x, zl, y, c)),
        (lax.rem(r + 2, 4), own_of(x, 1 - zl, y, c)),
    ]
    for s in range(1, 4):
        for k in range(2):
            rows = piece(0, k, *p12(k))
            send(
                wbuf.at[0, :, rows, :], wbuf.at[s, :, rows, :],
                wsem(), w1r.at[s - 1, k], zdest[s - 1],
            )

    def stage_direct(s, k, stg):
        p1, p2 = p12(k)
        axis = k if stg == 1 else 1 - k
        rows = piece(s, k, p1, p2) if stg == 1 else group(s, k, p2)
        sems = st1r if stg == 1 else st2r
        send(wbuf.at[s, :, rows, :], wbuf.at[s, :, rows, :], wsem(), sems.at[s - 1, k, 0], along(axis, 1))
        send(wbuf.at[s, :, rows, :], wbuf.at[s, :, rows, :], wsem(), sems.at[s - 1, k, 1], along(axis, -1))

    def rows_at(s, k, stg, d):
        p1, p2 = p12(k)
        return piece(s, k, near(p1, d), p2) if stg == 1 else group(s, k, near(p2, d))

    def stage_forward(s, k, stg):
        axis = k if stg == 1 else 1 - k
        sems = st1r if stg == 1 else st2r
        rm = rows_at(s, k, stg, -1)
        rp = rows_at(s, k, stg, 1)
        arrived(wbuf.at[s, :, rm, :], sems.at[s - 1, k, 0], along(axis, -1))
        send(wbuf.at[s, 0, rm, :], wbuf.at[s, 0, rm, :], wsem(), sems.at[s - 1, k, 2], along(axis, 1))
        arrived(wbuf.at[s, :, rp, :], sems.at[s - 1, k, 1], along(axis, 1))
        send(wbuf.at[s, 1, rp, :], wbuf.at[s, 1, rp, :], wsem(), sems.at[s - 1, k, 3], along(axis, -1))

    def stage_far(s, k, stg):
        axis = k if stg == 1 else 1 - k
        sems = st1r if stg == 1 else st2r
        rf = rows_at(s, k, stg, 2)
        arrived(wbuf.at[s, 0, rf, :], sems.at[s - 1, k, 2], along(axis, -1))
        arrived(wbuf.at[s, 1, rf, :], sems.at[s - 1, k, 3], along(axis, 1))

    def s1(s):
        for k in range(2):
            arrived(wbuf.at[s, :, piece(s, k, *p12(k)), :], w1r.at[s - 1, k], zpeer(1))
            stage_direct(s, k, 1)

    def f1(s):
        for k in range(2):
            stage_forward(s, k, 1)

    def s2(s):
        for k in range(2):
            stage_far(s, k, 1)
            stage_direct(s, k, 2)

    def f2(s):
        for k in range(2):
            stage_forward(s, k, 2)

    def d2d(s):
        for k in range(2):
            stage_far(s, k, 2)
            rows = pl.ds(pl.multiple_of(base(c, k), 512), 512)
            send(wbuf.at[s, :, rows, :], wbuf.at[s, :, rows, :], wsem(), ddr.at[s - 1, k], partner)

    def lift(s):
        loads[2 + 2 * s].wait()
        loads[3 + 2 * s].wait()

        def body(i, carry):
            cols = pl.ds(pl.multiple_of(quarter[s] * 2048 + i * 128, 128), 128)
            g = gcol[...]
            lv[:, cols] = (g * xv[:, cols].astype(F32) * lv[:, cols].astype(F32)).astype(BF16)
            return carry

        lax.fori_loop(0, 16, body, 0)

    def matmul(s, cc):
        rows = pl.ds(pl.multiple_of(cc * 1024, 1024), 1024)
        cols = pl.ds(pl.multiple_of(quarter[s] * 2048 + cc * 1024, 1024), 1024)
        pacc[0] += jnp.dot(xv[:, cols], wbuf[s, 0, rows, :], preferred_element_type=F32)
        pacc[1] += jnp.dot(lv[:, cols], wbuf[s, 1, rows, :], preferred_element_type=F32)

    gcol[...] = jnp.transpose(jnp.broadcast_to(gate_ref[...], (128, 256)))
    pacc[...] = jnp.zeros_like(pacc)
    s1(1)
    lift(0)
    s1(2)
    f1(1)
    lift(1)
    s1(3)
    f1(2)
    s2(1)
    matmul(0, c)
    f1(3)
    s2(2)
    matmul(0, 1 - c)
    f2(1)
    s2(3)
    lift(2)
    f2(2)
    d2d(1)
    lift(3)
    f2(3)
    matmul(1, c)
    d2d(2)
    matmul(2, c)

    def from_partner(s):
        for k in range(2):
            rows = pl.ds(pl.multiple_of(base(1 - c, k), 512), 512)
            arrived(wbuf.at[s, :, rows, :], ddr.at[s - 1, k], partner)
        matmul(s, 1 - c)

    from_partner(1)
    from_partner(2)
    d2d(3)
    matmul(3, c)
    from_partner(3)

    inner = jnp.tanh(pacc[0]).astype(BF16)
    outer = jnp.tanh(jnp.dot(inner, mix_ref[...], preferred_element_type=F32))
    slope = (pacc[1] * (1.0 - outer * outer)).astype(BF16)
    through = lax.dot_general(
        slope, mix_ref[...], (((1,), (1,)), ((), ())), preferred_element_type=F32
    )
    inner_wide = inner.astype(F32)
    signal = through * (1.0 - inner_wide * inner_wide)
    sigp[...] = jnp.transpose(signal).astype(BF16)
    other_rows = pl.ds(pl.multiple_of((1 - c) * 128, 128), 128)
    own_rows = pl.ds(pl.multiple_of(c * 128, 128), 128)

    ngs = [0]

    def gsem():
        ngs[0] += 1
        return gsend.at[ngs[0] - 1]

    for g in range(4):

        def grad(i, carry, g=g):
            b = g * 8 + i
            cols = pl.ds(pl.multiple_of(b * 256, 256), 256)
            xb = xv[:, cols]
            dsend[b] = jnp.dot(sigp[other_rows, :], xb, preferred_element_type=F32).astype(BF16)
            acc[b] = jnp.dot(sigp[own_rows, :], xb, preferred_element_type=F32)
            return carry

        lax.fori_loop(0, 8, grad, 0)
        blk = pl.ds(g * 8, 8)
        send(dsend.at[blk], drecv.at[blk], gsem(), gdr.at[g], partner)

    def rows16(k, d):
        i = near(pos[k], d)
        return pl.ds(pl.multiple_of(k * 64 + i * 16, 16), 16)

    for g in range(4):
        blk = pl.ds(g * 8, 8)
        arrived(drecv.at[blk], gdr.at[g], partner)

        def merge(i, carry, g=g):
            b = g * 8 + i
            acc[b] = acc[b] + drecv[b].astype(F32)
            for k in range(2):
                s1send[k, 0, b] = acc[b, rows16(k, 2), :].astype(BF16)
                d = 1 if g >= 2 else -1
                s1send[k, 1 if g >= 2 else 2, b] = acc[b, rows16(k, d), :].astype(BF16)
            return carry

        lax.fori_loop(0, 8, merge, 0)
        for k in range(2):
            if g < 2:
                send(s1send.at[k, 0, blk], s1rel.at[k, 0, blk], gsem(), s1relr.at[k, 0, g], along(k, 1))
                send(s1send.at[k, 2, blk], s1recv.at[k, 1, blk], gsem(), s1r.at[k, 1, g], along(k, -1))
            else:
                rel = pl.ds((g - 2) * 8, 8)
                send(s1send.at[k, 0, blk], s1rel.at[k, 1, rel], gsem(), s1relr.at[k, 1, g - 2], along(k, -1))
                send(s1send.at[k, 1, blk], s1recv.at[k, 0, blk], gsem(), s1r.at[k, 0, g], along(k, 1))

    for side in range(2):
        for h in range(2):
            g = 2 * side + h
            for k in range(2):
                blk = pl.ds(g * 8, 8)
                rel = pl.ds(h * 8, 8)
                d = 1 if side == 0 else -1
                arrived(s1rel.at[k, side, rel], s1relr.at[k, side, h], along(k, -d))

                def relay(i, carry, g=g, h=h, k=k, side=side, d=d):
                    b = g * 8 + i
                    s1send[k, 1 + side, b] = (
                        acc[b, rows16(k, d), :] + s1rel[k, side, h * 8 + i].astype(F32)
                    ).astype(BF16)
                    return carry

                lax.fori_loop(0, 8, relay, 0)
                send(s1send.at[k, 1 + side, blk], s1recv.at[k, side, blk], gsem(), s1r.at[k, side, g], along(k, d))

    for k in range(2):
        for g in (2, 3):
            arrived(s1recv.at[k, 0, pl.ds(g * 8, 8)], s1r.at[k, 0, g], along(k, -1))
        for g in (0, 1):
            arrived(s1recv.at[k, 1, pl.ds(g * 8, 8)], s1r.at[k, 1, g], along(k, 1))
    for k in range(2):
        for g in (0, 1):
            arrived(s1recv.at[k, 0, pl.ds(g * 8, 8)], s1r.at[k, 0, g], along(k, -1))
        for g in (2, 3):
            arrived(s1recv.at[k, 1, pl.ds(g * 8, 8)], s1r.at[k, 1, g], along(k, 1))

        def own_sum(i, carry, k=k):
            tot = []
            for q in range(2):
                b = i * 2 + q
                tot.append(
                    acc[b, rows16(k, 0), :]
                    + s1recv[k, 0, b].astype(F32)
                    + s1recv[k, 1, b].astype(F32)
                )
            rows = pl.ds(pl.multiple_of(i * 16, 16), 16)
            for j in range(4):
                a, h = j // 2, j % 2
                part = jnp.concatenate(
                    [t[a * 8 : a * 8 + 8, h * 128 : h * 128 + 128] for t in tot], axis=0
                )
                s2f[k, j, rows, :] = part
                s2send[k, j, rows, :] = part.astype(BF16)
            return carry

        lax.fori_loop(0, 16, own_sum, 0)
        for d in (1, 3, 2):
            j = near(pos[1 - k], d)
            send(s2send.at[k, j], s2recv.at[k, d - 1], gsem(), s2r.at[k, d - 1], along(1 - k, d))

    parts = []
    for k in range(2):
        tot = s2f[k, pos[1 - k]]
        for d in (1, 3, 2):
            arrived(s2recv.at[k, d - 1], s2r.at[k, d - 1], along(1 - k, -d))
            tot = tot + s2recv[k, d - 1].astype(F32)
        parts.append(tot.reshape(32, 8, 128))
    both = jnp.concatenate(parts, axis=1)
    zf[...] = both
    zsend[...] = both.astype(BF16)

    for d in (4, 3, 5, 2, 6, 1, 7):
        zz = lax.rem(z + d, 8)
        send(zsend.at[pl.ds(zz * 4, 4)], zrecv.at[d - 1], gsem(), zr.at[d - 1], zpeer(d))
    tot = zf[pl.ds(z * 4, 4)]
    for d in (1, 7, 2, 6, 3, 5, 4):
        arrived(zrecv.at[d - 1], zr.at[d - 1], zpeer(-d))
        tot = tot + zrecv[d - 1].astype(F32)
    mine = pl.ds(z * 4, 4)
    zag[mine] = tot.astype(BF16)
    for d in (4, 3, 5, 2, 6, 1, 7):
        send(zag.at[mine], zag.at[mine], gsem(), zagr.at[d - 1], zpeer(d))
    for d in (1, 7, 2, 6, 3, 5, 4):
        zz = lax.rem(z - d + 8, 8)
        arrived(zag.at[pl.ds(zz * 4, 4)], zagr.at[d - 1], zpeer(-d))

    def choose(mm, carry):
        _, oo = plane(mm)
        stage[mm] = zag[jnp.maximum(table_ref[oo], 0)]
        return carry

    lax.fori_loop(0, 32, choose, 0)

    def to_owner(e):
        mm = lax.rem(m + e, 32)
        return pltpu.make_async_remote_copy(
            src_ref=stage.at[mm], dst_ref=arecv.at[m], send_sem=asend.at[e - 1],
            recv_sem=ar.at[e - 1], device_id=plane(mm), device_id_type=MESH,
        )

    def go(e, carry):
        to_owner(e).start()
        return carry

    lax.fori_loop(1, 32, go, 0)
    arecv[m] = stage[m]

    def land(e, carry):
        mm = lax.rem(m - e + 32, 32)
        arrived(arecv.at[mm], ar.at[e - 1], plane(mm))
        return carry

    lax.fori_loop(1, 32, land, 0)
    for xx in range(4):
        for yy in range(4):
            for cc in range(2):
                tile = arecv[(xx * 4 + yy) * 2 + cc].astype(F32)
                r0 = cc * 128 + xx * 16 + (yy // 2) * 8
                l0 = (yy % 2) * 128
                out_ref[r0 : r0 + 8, l0 : l0 + 128] = tile[0:8]
                r1 = cc * 128 + 64 + yy * 16 + (xx // 2) * 8
                l1 = (xx % 2) * 128
                out_ref[r1 : r1 + 8, l1 : l1 + 128] = tile[8:16]

    def drain(e, carry):
        to_owner(e).wait_send()
        return carry

    lax.fori_loop(1, 32, drain, 0)
    for cp in pending:
        cp.wait_send()


def reduced_block(inputs, cotangent, gate, down_weight, up_weight, mixing, table):
    any_spec = pl.BlockSpec(memory_space=pl.ANY)
    vm = pl.BlockSpec(memory_space=pltpu.VMEM)
    dma = pltpu.SemaphoreType.DMA
    V = pltpu.VMEM
    return pl.pallas_call(
        reduce_kernel,
        name="reduce",
        out_shape=jax.ShapeDtypeStruct((256, 256), F32),
        in_specs=[any_spec, any_spec, vm, any_spec, any_spec, vm,
                  pl.BlockSpec(memory_space=pltpu.SMEM)],
        out_specs=vm,
        scratch_shapes=[
            V((4, 2, 2048, 256), BF16),
            V((256, 8192), BF16),
            V((256, 8192), BF16),
            V((256, 128), F32),
            V((2, 256, 256), F32),
            V((256, 256), BF16),
            V((32, 128, 256), BF16),
            V((32, 128, 256), BF16),
            V((32, 128, 256), F32),
            V((2, 3, 32, 16, 256), BF16),
            V((2, 2, 16, 16, 256), BF16),
            V((2, 2, 32, 16, 256), BF16),
            V((2, 4, 256, 128), F32),
            V((2, 4, 256, 128), BF16),
            V((2, 3, 256, 128), BF16),
            V((32, 16, 128), F32),
            V((32, 16, 128), BF16),
            V((7, 4, 16, 128), BF16),
            V((32, 16, 128), BF16),
            V((32, 16, 128), BF16),
            V((32, 16, 128), BF16),
            dma((10,)),
            dma((60,)),
            dma((3, 2)),
            dma((3, 2, 4)),
            dma((3, 2, 4)),
            dma((3, 2)),
            dma((48,)),
            dma((4,)),
            dma((2, 2, 2)),
            dma((2, 2, 4)),
            dma((2, 3)),
            dma((7,)),
            dma((7,)),
            dma((31,)),
            dma((31,)),
        ],
        compiler_params=pltpu.CompilerParams(
            collective_id=0, has_side_effects=True, vmem_limit_bytes=56 * 1024 * 1024
        ),
    )(inputs, cotangent, gate, down_weight, up_weight, mixing, table)


def halves(a):
    hi = a.astype(BF16)
    return hi, (a - hi.astype(F32)).astype(BF16)


def product(a, b):
    (ah, al), (bh, bl) = a, b
    lhs = jnp.concatenate([ah, ah, al], axis=1)
    rhs = jnp.concatenate([bh, bl, bh], axis=0)
    return jnp.dot(lhs, rhs, preferred_element_type=F32)


def root_kernel(gt_ref, left_ref, right_ref, table_ref, out_ref):
    eye = (
        lax.broadcasted_iota(jnp.int32, (R, R), 0) == lax.broadcasted_iota(jnp.int32, (R, R), 1)
    ).astype(F32)
    gt = gt_ref[...] * (1.0 / TOKENS)
    gs = halves(jnp.transpose(gt))
    gts = halves(gt)
    news = [
        BETA * left_ref[0] + (1.0 - BETA) * product(gs, gts),
        BETA * right_ref[0] + (1.0 - BETA) * product(gts, gs),
    ]
    results, norms = [], []
    for a in news:
        shifted = a + EPS * eye
        total = jnp.sum(shifted * shifted, keepdims=True)
        norm = jnp.sqrt(total)
        results.append(lax.rsqrt(jnp.sqrt(norm)))
        norms.append(shifted / norm)
    for sweep in range(ITERS):
        for i in range(2):
            factor = (5.0 * eye - norms[i]) / 4.0
            fs = halves(factor)
            if sweep == 0:
                results[i] = results[i] * factor
            else:
                results[i] = product(halves(results[i]), fs)
            if sweep < ITERS - 1:
                ss = halves(product(fs, fs))
                ms = halves(norms[i])
                norms[i] = product(halves(product(ss, ss)), ms)
    done = product(halves(product(halves(results[0]), gs)), halves(results[1]))
    filled = table_ref[lax.axis_index("own")] >= 0
    out_ref[...] = jnp.where(filled, done, 0.0)


def preconditioned(gt, left, right, table):
    vm = pl.BlockSpec(memory_space=pltpu.VMEM)
    return pl.pallas_call(
        root_kernel,
        name="roots",
        out_shape=jax.ShapeDtypeStruct((R, R), F32),
        in_specs=[vm, vm, vm, pl.BlockSpec(memory_space=pltpu.SMEM)],
        out_specs=vm,
    )(gt, left, right, table)


def shards(
    inputs, cotangent, gate, down_weight, up_weight, mixing, owner_table, left_factor, right_factor
):
    table = owner_table.reshape(-1)
    gt = reduced_block(
        inputs, cotangent, gate.reshape(1, -1), down_weight, up_weight, mixing, table
    )
    return preconditioned(gt, left_factor, right_factor, table)


def solution(mesh):
    in_specs = (
        P(("rep", "own"), None),
        P(("rep", "own"), None),
        P(("rep", "own")),
        P("rep", None),
        P("rep", None),
        P(),
        P(),
        P("own", None, None),
        P("own", None, None),
    )
    return jax.shard_map(
        shards, mesh=mesh, in_specs=in_specs, out_specs=P("own", None), check_vma=False
    )
```

time: 413 us -> 94.6 us (0.23)
  waiting for transfers between devices: 271 us -> 0 us
  Pallas kernels: 0 us -> 94.5 us
  blocking collectives: 89.5 us -> 0 us
  matrix products: 29.4 us -> 0 us
  between operations: 14.7 us -> 0.01 us
  local copies, waits for them, and re-layouts: 5.69 us -> 0 us
    all_gather x3 -> x0, waiting for transfers between devices: 269 us -> none  [the longest x1 107 us: shards(): shard_rows = lax.all_gather(shard, 'own', axis=0, tiled=True)]
    pallas_call x0 -> x2, Pallas kernels: none -> 94.5 us  [the longest x1 85.3 us: reduced_block(): pl.pallas_call(reduce_kernel, name='reduce', out_shape=jax.ShapeDtypeStru...]
    all_to_all x2 -> x0, blocking collectives: 89.5 us -> none  [the longest x1 71.1 us: sent_and_summed(): lax.all_to_all(parts, axis, split_axis=0, concat_axis=0, tiled=True)]
    dot_general x25 -> x0, matrix products: 29.4 us -> none  [the longest x21 14.8 us: batched(): jnp.einsum('kij,kjl->kil', left, right, precision=lax.Precision.HIGHEST)]
    gather x1 -> x0, local copies, waits for them, and re-layouts: 4.34 us -> none  [shards(): selected = jnp.take(shard_rows, jnp.clip(wanted, 0, row_total - 1), axis=0)]
  transfers between devices with their start and end apart: 3 -> 0, of which waited for: 3 -> 0; matrix products, arithmetic and copies ran while one was open for 1% -> 0% of each run, Pallas kernels for 0% -> 0%
where the time goes in v1:
time: 94.6 us; the launch traced here: 94.5 us
  Pallas kernels  94.5 us (100%)
    pallas_call x1, Pallas kernels, reduced_block(): pl.pallas_call(reduce_kernel, name='reduce', out_shape=jax.ShapeDtypeStru...  85.3 us
    pallas_call x1, Pallas kernels, preconditioned(): pl.pallas_call(root_kernel, name='roots', out_shape=jax.ShapeDtypeStruct(...  9.2 us

profile of v1, /device:TPU:1, one launch (start us, length us, event | category | flops | bytes accessed | tf_op | source)
XLA Modules:
  0.0 94.5 jit_solution(10383608254863315984)
XLA Ops:
  0.0 85.3 %reduce.1.gt_ref = f32[256,256]{1,0:T(8,128)} custom-call(bf16[256,8192]{1,0:T(8,128)(2,1)} %x_hbm.1, bf16[256,8192]{1,0:T(8,128)(2,1)} %cot_hbm.1, f32[1,256]{1,0:T(1,128)} %bitcast.4, bf16[2048,256]{1,0:T(8,128)(2,1)} %down_hbm.1, bf16[2048,256]{1,0:T(8,128)(2,1)} %up_hbm.1, bf16[256,256]{1,0:T(8,128)(2,1)} %mix_ref.1, s32[64]{0:T(128)} %bitcast.2), custom_call_target="tpu_custom_call" | custom-call | tf_op jit(solution)/shard_map/reduce/pallas_call | solution.py:436
  85.3 9.2 %roots.1 = f32[256,256]{1,0:T(8,128)} custom-call(f32[256,256]{1,0:T(8,128)} %reduce.1.gt_ref, f32[1,256,256]{2,1,0:T(8,128)} %left_ref.1, f32[1,256,256]{2,1,0:T(8,128)} %right_ref.1, s32[64]{0:T(128)} %bitcast.3), custom_call_target="tpu_custom_call" | custom-call | tf_op jit(solution)/shard_map/roots/pallas_call | solution.py:536

commit v2 on v1

v2 whole, which is shorter than its diff:
```python
import functools

import jax
import jax.numpy as jnp
from jax import lax
from jax.experimental import pallas as pl
from jax.experimental.pallas import tpu as pltpu
from jax.sharding import PartitionSpec as P

R = 256
ITERS = 5
BETA = 0.95
EPS = 1e-06
TOKENS = 65536

F32 = jnp.float32
BF16 = jnp.bfloat16
MESH = pl.DeviceIdType.MESH


def own_of(x, zl, y, c):
    return ((x * 2 + zl) * 4 + y) * 2 + c


def reduce_kernel(
    x_hbm, cot_hbm, gate_ref, down_hbm, up_hbm, mix_ref, table_ref, out_ref,
    wbuf, xv, lv, gcol, pacc, sigp, sigr, xp, acc,
    s1send, s1rel, s1recv, s2f, s2send, s2recv, zf, zsend, zrecv, zag, stage, arecv,
    ld, wsend, w1r, st1r, st2r, zp1, zp2, ddr, xr, gsend, gdr, s1relr, s1r, s2r, zr, zagr, asend, ar,
):
    r = lax.axis_index("rep")
    o = lax.axis_index("own")
    c = lax.rem(o, 2)
    y = lax.rem(o // 2, 4)
    zl = lax.rem(o // 8, 2)
    x = o // 16
    z = r * 2 + zl
    m = (x * 4 + y) * 2 + c
    sgn = 2 * zl - 1
    partner = (r, own_of(x, zl, y, 1 - c))

    xs = [lax.rem(x + d, 4) for d in range(4)]
    ys = [lax.rem(y + d, 4) for d in range(4)]
    cs = [c, 1 - c]
    x_part = [v * 16 + zl * 8 for v in xs]
    y_part = [v * 2 for v in ys]
    zs = [lax.rem(z + d, 8) for d in range(8)]

    def along(axis, d):
        if axis == 0:
            return (r, x_part[d % 4] + y_part[0] + c)
        return (r, x_part[0] + y_part[d % 4] + c)

    def zpeer(d):
        zz = zs[d % 8]
        return (lax.div(zz, 2), x * 16 + lax.rem(zz, 2) * 8 + y_part[0] + c)

    def plane(dx, dy, dc):
        return (r, x_part[dx % 4] + y_part[dy % 4] + cs[dc])

    def place(dx, dy, dc):
        return xs[dx % 4] * 8 + y_part[dy % 4] + cs[dc]

    def length(d):
        return min(d, 4 - d)

    offsets = [(dx, dy, dc) for dx in range(4) for dy in range(4) for dc in range(2)][1:]
    offsets.sort(key=lambda t: -(length(t[0]) + length(t[1])))

    quarter = [r, lax.rem(r + sgn + 4, 4), lax.rem(r - sgn + 4, 4), lax.rem(r + 2, 4)]

    pending = []

    def send(src, dst, ssem, rsem, dev):
        cp = pltpu.make_async_remote_copy(
            src_ref=src, dst_ref=dst, send_sem=ssem, recv_sem=rsem,
            device_id=dev, device_id_type=MESH,
        )
        cp.start()
        pending.append(cp)

    def arrived(dst, rsem, dev):
        pltpu.make_async_remote_copy(
            src_ref=dst, dst_ref=dst, send_sem=rsem, recv_sem=rsem,
            device_id=dev, device_id_type=MESH,
        ).wait_recv()

    loads = [
        pltpu.make_async_copy(down_hbm, wbuf.at[0, 0], ld.at[0]),
        pltpu.make_async_copy(up_hbm, wbuf.at[0, 1], ld.at[1]),
    ]
    for s in range(4):
        cols = pl.ds(pl.multiple_of(quarter[s] * 2048, 2048), 2048)
        loads.append(pltpu.make_async_copy(x_hbm.at[:, cols], xv.at[:, cols], ld.at[2 + 2 * s]))
        loads.append(pltpu.make_async_copy(cot_hbm.at[:, cols], lv.at[:, cols], ld.at[3 + 2 * s]))
    for cp in loads:
        cp.start()

    barrier = pltpu.get_barrier_semaphore()

    for d in (4, 3, 5):
        pl.semaphore_signal(barrier, inc=1, device_id=zpeer(d), device_id_type=MESH)
    for off in offsets:
        pl.semaphore_signal(barrier, inc=1, device_id=plane(*off), device_id_type=MESH)
    for d in (2, 6, 1, 7):
        pl.semaphore_signal(barrier, inc=1, device_id=zpeer(d), device_id_type=MESH)
    pl.semaphore_wait(barrier, 38)

    pos = (x, y)
    nws = [0]

    def wsem():
        nws[0] += 1
        return wsend.at[nws[0] - 1]

    def unit(s, k):
        return 16 if (s, k) in ((1, 1), (2, 0)) else 32

    def base(s, cc, k):
        return cc * 1024 + (16 * unit(s, 0) if k else 0)

    def piece(s, k, p1, p2):
        u = unit(s, k)
        return pl.ds(pl.multiple_of(base(s, c, k) + (p2 * 4 + p1) * u, u), u)

    def group(s, k, p2):
        u = 4 * unit(s, k)
        return pl.ds(pl.multiple_of(base(s, c, k) + p2 * u, u), u)

    def straight(cc, n):
        return pl.ds(pl.multiple_of(cc * 1024 + 768 + n * 64, 64), 64)

    def p12(k):
        return (pos[0], pos[1]) if k == 0 else (pos[1], pos[0])

    def near(p, d):
        return lax.rem(p + d + 4, 4)

    loads[0].wait()
    loads[1].wait()
    zdest = [
        (lax.rem(r + sgn + 4, 4), own_of(x, 1 - zl, y, c)),
        (lax.rem(r + sgn + 4, 4), own_of(x, zl, y, c)),
        (lax.rem(r + 2, 4), own_of(x, 1 - zl, y, c)),
    ]
    for s in (3, 1, 2):
        for k in range(2):
            rows = piece(s, k, *p12(k))
            send(
                wbuf.at[0, :, rows, :], wbuf.at[s, :, rows, :],
                wsem(), w1r.at[s - 1, k], zdest[s - 1],
            )
    for n in range(4):
        rows = straight(c, n)
        send(wbuf.at[0, :, rows, :], wbuf.at[1, :, rows, :], wsem(), zp1.at[n], zdest[0])
    pair = (r, own_of(x, 1 - zl, y, c))

    def pass_on(n):
        rows = straight(c, n)
        arrived(wbuf.at[1, :, rows, :], zp1.at[n], pair)
        send(wbuf.at[1, :, rows, :], wbuf.at[2, :, rows, :], wsem(), zp2.at[n], pair)

    def rows_at(s, k, stg, d):
        p1, p2 = p12(k)
        return piece(s, k, near(p1, d), p2) if stg == 1 else group(s, k, near(p2, d))

    def s1(s):
        for k in range(2):
            rows = rows_at(s, k, 1, 0)
            arrived(wbuf.at[s, :, rows, :], w1r.at[s - 1, k], zpeer(1))
            for d in (2, 1, 3):
                send(
                    wbuf.at[s, :, rows, :], wbuf.at[s, :, rows, :],
                    wsem(), st1r.at[s - 1, k, d], along(k, d),
                )

    def s2(s):
        for k in range(2):
            for d in (1, 3, 2):
                arrived(wbuf.at[s, :, rows_at(s, k, 1, -d), :], st1r.at[s - 1, k, d], along(k, -d))
        for k in range(2):
            rows = rows_at(s, k, 2, 0)
            for i, d in enumerate((1, 3)):
                send(
                    wbuf.at[s, :, rows, :], wbuf.at[s, :, rows, :],
                    wsem(), st2r.at[s - 1, k, i], along(1 - k, d),
                )

    def f2(s):
        for k in range(2):
            for i, d in enumerate((1, 3)):
                rows = rows_at(s, k, 2, -d)
                arrived(wbuf.at[s, :, rows, :], st2r.at[s - 1, k, i], along(1 - k, -d))
                send(
                    wbuf.at[s, i, rows, :], wbuf.at[s, i, rows, :],
                    wsem(), st2r.at[s - 1, k, 2 + i], along(1 - k, d),
                )

    def stage_far(s, k):
        rows = rows_at(s, k, 2, 2)
        for i, d in enumerate((1, 3)):
            arrived(wbuf.at[s, i, rows, :], st2r.at[s - 1, k, 2 + i], along(1 - k, -d))

    def to_partner(s, rows, i):
        send(wbuf.at[s, :, rows, :], wbuf.at[s, :, rows, :], wsem(), ddr.at[i], partner)

    def gathered(cc):
        return pl.ds(pl.multiple_of(cc * 1024, 256), 768)

    def d2d(s):
        for k in range(2):
            stage_far(s, k)
        to_partner(s, gathered(c), s - 1)

    def d2d_straight1():
        to_partner(1, pl.ds(pl.multiple_of(c * 1024 + 768, 256), 256), 2)

    def d2d_straight2(n):
        arrived(wbuf.at[2, :, straight(c, n), :], zp2.at[n], pair)
        to_partner(2, straight(c, n), 3 + n)

    def d2d_last(far):
        for k in range(2):
            if far:
                stage_far(3, k)
            for i, d in ((3, 2),) if far else ((0, 0), (1, -1), (2, 1)):
                to_partner(3, rows_at(3, k, 2, d), 7 + k * 4 + i)

    def from_partner(s):
        if s < 3:
            arrived(wbuf.at[s, :, gathered(1 - c), :], ddr.at[s - 1], partner)
        if s == 1:
            rows = pl.ds(pl.multiple_of((1 - c) * 1024 + 768, 256), 256)
            arrived(wbuf.at[1, :, rows, :], ddr.at[2], partner)
        if s == 2:
            for n in range(4):
                arrived(wbuf.at[2, :, straight(1 - c, n), :], ddr.at[3 + n], partner)
        if s == 3:
            for k in range(2):
                for i, d in enumerate((0, -1, 1, 2)):
                    _, p2 = p12(k)
                    rows = pl.ds(
                        pl.multiple_of(base(3, 1 - c, k) + near(p2, d) * 128, 128), 128
                    )
                    arrived(wbuf.at[3, :, rows, :], ddr.at[7 + k * 4 + i], partner)
        matmul(s, 1 - c)

    def cols_of(s):
        return pl.ds(pl.multiple_of(quarter[s] * 2048, 2048), 2048)

    def share(s):
        loads[2 + 2 * s].wait()
        send(xv.at[:, cols_of(s)], xp.at[:, cols_of(s)], wsem(), xr.at[s], partner)

    def lift(s, first, last):
        if first == 0:
            loads[3 + 2 * s].wait()

        def body(i, carry):
            cols = pl.ds(pl.multiple_of(quarter[s] * 2048 + i * 128, 128), 128)
            g = gcol[...]
            lv[:, cols] = (g * xv[:, cols].astype(F32) * lv[:, cols].astype(F32)).astype(BF16)
            return carry

        lax.fori_loop(first, last, body, 0)

    def matmul(s, cc):
        def body(i, carry):
            start = cc * 1024 + i * 512
            rows = pl.ds(pl.multiple_of(start, 512), 512)
            cols = pl.ds(pl.multiple_of(quarter[s] * 2048 + start, 512), 512)
            pacc[0] += jnp.dot(xv[:, cols], wbuf[s, 0, rows, :], preferred_element_type=F32)
            pacc[1] += jnp.dot(lv[:, cols], wbuf[s, 1, rows, :], preferred_element_type=F32)
            return carry

        lax.fori_loop(0, 2, body, 0)

    gcol[...] = jnp.transpose(jnp.broadcast_to(gate_ref[...], (128, 256)))
    pacc[...] = jnp.zeros_like(pacc)
    for s in range(4):
        share(s)
    lift(0, 0, 8)
    s1(1)
    s1(2)
    lift(0, 8, 16)
    s1(3)
    s2(1)
    pass_on(0)
    s2(2)
    pass_on(1)
    lift(1, 0, 8)
    pass_on(2)
    s2(3)
    pass_on(3)
    f2(1)
    d2d_straight1()
    lift(1, 8, 16)
    matmul(0, c)
    d2d_straight2(0)
    d2d_straight2(1)
    f2(2)
    lift(2, 0, 16)
    d2d_straight2(2)
    d2d_straight2(3)
    matmul(0, 1 - c)
    f2(3)
    d2d_last(False)
    lift(3, 0, 8)
    d2d(1)
    matmul(1, c)
    lift(3, 8, 16)
    d2d(2)
    matmul(2, c)
    from_partner(1)
    d2d_last(True)
    matmul(3, c)
    from_partner(2)
    from_partner(3)

    inner = jnp.tanh(pacc[0]).astype(BF16)
    outer = jnp.tanh(jnp.dot(inner, mix_ref[...], preferred_element_type=F32))
    slope = (pacc[1] * (1.0 - outer * outer)).astype(BF16)
    through = lax.dot_general(
        slope, mix_ref[...], (((1,), (1,)), ((), ())), preferred_element_type=F32
    )
    inner_wide = inner.astype(F32)
    signal = through * (1.0 - inner_wide * inner_wide)
    sigp[...] = jnp.transpose(signal).astype(BF16)
    other_rows = pl.ds(pl.multiple_of((1 - c) * 128, 128), 128)
    own_rows = pl.ds(pl.multiple_of(c * 128, 128), 128)

    ngs = [0]

    def gsem():
        ngs[0] += 1
        return gsend.at[ngs[0] - 1]

    send(sigp.at[other_rows], sigr, gsem(), gdr, partner)

    def own_tokens(i, carry):
        cols = pl.ds(pl.multiple_of(i * 256, 256), 256)
        acc[i] = jnp.dot(sigp[own_rows, :], xv[:, cols], preferred_element_type=F32)
        return carry

    lax.fori_loop(0, 32, own_tokens, 0, unroll=4)
    for s in range(4):
        arrived(xp.at[:, cols_of(s)], xr.at[s], partner)
    arrived(sigr, gdr, partner)

    def rows16(k, d):
        i = near(pos[k], d)
        return pl.ds(pl.multiple_of(k * 64 + i * 16, 16), 16)

    def merge(g):
        role, d = (2, -1) if g % 2 == 0 else (1, 1)

        def body(i, carry):
            b = g * 8 + i
            cols = pl.ds(pl.multiple_of(b * 256, 256), 256)
            acc[b] += jnp.dot(sigr[...], xp[:, cols], preferred_element_type=F32)
            for k in range(2):
                s1send[k, 0, b] = acc[b, rows16(k, 2), :].astype(BF16)
                s1send[k, role, b] = acc[b, rows16(k, d), :].astype(BF16)
            return carry

        lax.fori_loop(0, 8, body, 0, unroll=4)

    def far_out(g):
        side, rnd = g % 2, g // 2
        blk, rel = pl.ds(g * 8, 8), pl.ds(rnd * 8, 8)
        for k in range(2):
            send(
                s1send.at[k, 0, blk], s1rel.at[k, side, rel], gsem(),
                s1relr.at[k, side, rnd], along(k, 1 - 2 * side),
            )

    def near_out(g, role):
        blk = pl.ds(g * 8, 8)
        for k in range(2):
            send(
                s1send.at[k, role, blk], s1recv.at[k, role - 1, blk], gsem(),
                s1r.at[k, role - 1, g], along(k, 3 - 2 * role),
            )

    def relay(g):
        side, rnd = g % 2, g // 2
        rel = pl.ds(rnd * 8, 8)
        d = 1 - 2 * side
        for k in range(2):
            arrived(s1rel.at[k, side, rel], s1relr.at[k, side, rnd], along(k, -d))

            def body(i, carry, k=k):
                b = g * 8 + i
                s1send[k, 1 + side, b] = (
                    acc[b, rows16(k, d), :] + s1rel[k, side, rnd * 8 + i].astype(F32)
                ).astype(BF16)
                return carry

            lax.fori_loop(0, 8, body, 0)
        near_out(g, 1 + side)

    def finish(rnd):
        half = pl.ds(rnd * 128, 128)
        for k in range(2):
            for role in range(2):
                for g in (2 * rnd, 2 * rnd + 1):
                    arrived(
                        s1recv.at[k, role, pl.ds(g * 8, 8)], s1r.at[k, role, g],
                        along(k, 2 * role - 1),
                    )

            def own_sum(i, carry, k=k):
                tot = []
                for q in range(2):
                    b = i * 2 + q
                    tot.append(
                        acc[b, rows16(k, 0), :]
                        + s1recv[k, 0, b].astype(F32)
                        + s1recv[k, 1, b].astype(F32)
                    )
                rows = pl.ds(pl.multiple_of(i * 16, 16), 16)
                for j in range(4):
                    a, h = j // 2, j % 2
                    part = jnp.concatenate(
                        [t[a * 8 : a * 8 + 8, h * 128 : h * 128 + 128] for t in tot], axis=0
                    )
                    s2f[k, j, rows, :] = part
                    s2send[k, j, rows, :] = part.astype(BF16)
                return carry

            lax.fori_loop(rnd * 8, rnd * 8 + 8, own_sum, 0)
            for d in (2, 1, 3):
                j = near(pos[1 - k], d)
                send(
                    s2send.at[k, j, half], s2recv.at[k, d - 1, half], gsem(),
                    s2r.at[k, d - 1, rnd], along(1 - k, d),
                )

    merge(0)
    far_out(0)
    near_out(0, 2)
    merge(1)
    far_out(1)
    near_out(1, 1)
    merge(2)
    far_out(2)
    merge(3)
    far_out(3)
    relay(0)
    near_out(3, 1)
    relay(1)
    near_out(2, 2)
    relay(2)
    finish(0)
    relay(3)
    finish(1)

    parts = []
    for k in range(2):
        tot = s2f[k, pos[1 - k]]
        for d in (1, 3, 2):
            for rnd in range(2):
                half = pl.ds(rnd * 128, 128)
                arrived(s2recv.at[k, d - 1, half], s2r.at[k, d - 1, rnd], along(1 - k, -d))
            tot = tot + s2recv[k, d - 1].astype(F32)
        parts.append(tot.reshape(32, 8, 128))
    both = jnp.concatenate(parts, axis=1)
    zf[...] = both
    zsend[...] = both.astype(BF16)

    for d in (4, 3, 5, 2, 6, 1, 7):
        zz = lax.rem(z + d, 8)
        send(zsend.at[pl.ds(zz * 4, 4)], zrecv.at[d - 1], gsem(), zr.at[d - 1], zpeer(d))
    tot = zf[pl.ds(z * 4, 4)]
    for d in (1, 7, 2, 6, 3, 5, 4):
        arrived(zrecv.at[d - 1], zr.at[d - 1], zpeer(-d))
        tot = tot + zrecv[d - 1].astype(F32)
    mine = pl.ds(z * 4, 4)
    zag[mine] = tot.astype(BF16)
    for d in (4, 3, 5, 2, 6, 1, 7):
        send(zag.at[mine], zag.at[mine], gsem(), zagr.at[d - 1], zpeer(d))
    for d in (1, 7, 2, 6, 3, 5, 4):
        zz = lax.rem(z - d + 8, 8)
        arrived(zag.at[pl.ds(zz * 4, 4)], zagr.at[d - 1], zpeer(-d))

    for e, off in enumerate(offsets):
        stage[e] = zag[jnp.maximum(table_ref[plane(*off)[1]], 0)]
    arecv[m] = zag[jnp.maximum(table_ref[o], 0)]
    for e, off in enumerate(offsets):
        pltpu.make_async_remote_copy(
            src_ref=stage.at[e], dst_ref=arecv.at[m], send_sem=asend, recv_sem=ar.at[e],
            device_id=plane(*off), device_id_type=MESH,
        ).start()
    for cp in pending:
        cp.wait_send()
    for e, (dx, dy, dc) in reversed(list(enumerate(offsets))):
        arrived(arecv.at[place(-dx, -dy, dc)], ar.at[e], plane(-dx, -dy, dc))
    for xx in range(4):
        for yy in range(4):
            for cc in range(2):
                tile = arecv[(xx * 4 + yy) * 2 + cc]
                r0 = cc * 128 + xx * 16 + (yy // 2) * 8
                l0 = (yy % 2) * 128
                out_ref[r0 : r0 + 8, l0 : l0 + 128] = tile[0:8]
                r1 = cc * 128 + 64 + yy * 16 + (xx // 2) * 8
                l1 = (xx % 2) * 128
                out_ref[r1 : r1 + 8, l1 : l1 + 128] = tile[8:16]

    first = pl.ds(0, 31)
    pltpu.make_async_remote_copy(
        src_ref=stage.at[first], dst_ref=arecv.at[first], send_sem=asend, recv_sem=asend,
        device_id=partner, device_id_type=MESH,
    ).wait_send()


def reduced_block(inputs, cotangent, gate, down_weight, up_weight, mixing, table):
    any_spec = pl.BlockSpec(memory_space=pltpu.HBM)
    vm = pl.BlockSpec(memory_space=pltpu.VMEM)
    dma = pltpu.SemaphoreType.DMA
    V = pltpu.VMEM
    return pl.pallas_call(
        reduce_kernel,
        name="reduce",
        out_shape=jax.ShapeDtypeStruct((256, 256), BF16),
        in_specs=[any_spec, any_spec, vm, any_spec, any_spec, vm,
                  pl.BlockSpec(memory_space=pltpu.SMEM)],
        out_specs=vm,
        scratch_shapes=[
            V((4, 2, 2048, 256), BF16),
            V((256, 8192), BF16),
            V((256, 8192), BF16),
            V((256, 128), F32),
            V((2, 256, 256), F32),
            V((256, 256), BF16),
            V((128, 256), BF16),
            V((256, 8192), BF16),
            V((32, 128, 256), F32),
            V((2, 3, 32, 16, 256), BF16),
            V((2, 2, 16, 16, 256), BF16),
            V((2, 2, 32, 16, 256), BF16),
            V((2, 4, 256, 128), F32),
            V((2, 4, 256, 128), BF16),
            V((2, 3, 256, 128), BF16),
            V((32, 16, 128), F32),
            V((32, 16, 128), BF16),
            V((7, 4, 16, 128), BF16),
            V((32, 16, 128), BF16),
            V((32, 16, 128), BF16),
            V((32, 16, 128), BF16),
            dma((10,)),
            dma((94,)),
            dma((3, 2)),
            dma((3, 2, 4)),
            dma((3, 2, 4)),
            dma((4,)),
            dma((4,)),
            dma((15,)),
            dma((4,)),
            dma((54,)),
            dma,
            dma((2, 2, 2)),
            dma((2, 2, 4)),
            dma((2, 3, 2)),
            dma((7,)),
            dma((7,)),
            dma,
            dma((31,)),
        ],
        compiler_params=pltpu.CompilerParams(
            collective_id=0, has_side_effects=True, vmem_limit_bytes=63 * 1024 * 1024
        ),
    )(inputs, cotangent, gate, down_weight, up_weight, mixing, table)


def halves(a):
    hi = a.astype(BF16)
    return hi, (a - hi.astype(F32)).astype(BF16)


def dot(a, b):
    return jnp.dot(a, b, preferred_element_type=F32)


def product(a, b):
    (ah, al), (bh, bl) = a, b
    lhs = jnp.concatenate([ah, ah, al], axis=1)
    rhs = jnp.concatenate([bh, bl, bh], axis=0)
    return dot(lhs, rhs)


def root_kernel(gt_ref, left_ref, right_ref, table_ref, out_ref, norms, results):
    eye = (
        lax.broadcasted_iota(jnp.int32, (R, R), 0) == lax.broadcasted_iota(jnp.int32, (R, R), 1)
    ).astype(F32)
    scaled = gt_ref[...].astype(F32) * (1.0 / TOKENS)
    gt = scaled.astype(BF16)
    g = jnp.transpose(scaled).astype(BF16)
    news = [
        BETA * left_ref[0] + (1.0 - BETA) * dot(g, gt),
        BETA * right_ref[0] + (1.0 - BETA) * dot(gt, g),
    ]
    for i, a in enumerate(news):
        shifted = a + EPS * eye
        norm = jnp.sqrt(jnp.sum(shifted * shifted, keepdims=True))
        m = shifted / norm
        results[i] = lax.rsqrt(jnp.sqrt(norm)) * ((5.0 * eye - m) / 4.0)
        norms[i] = m

    def advance(m, mb):
        e = dot(mb, mb) * (1.0 / 16.0) - m * (10.0 / 16.0)
        eb = e.astype(BF16)
        h = (25.0 / 8.0) * e + dot(eb, eb)
        return (625.0 / 256.0) * m + dot(h.astype(BF16), mb)

    def multiply(x, mb):
        return 1.25 * x - 0.25 * dot(x.astype(BF16), mb)

    for i in range(2):
        norms[i] = advance(norms[i], norms[i].astype(BF16))

    def sweep(step, carry):
        for i in range(2):
            m = norms[i]
            mb = m.astype(BF16)
            results[i] = multiply(results[i], mb)
            norms[i] = advance(m, mb)
        return carry

    lax.fori_loop(0, ITERS - 2, sweep, 0)
    left, right = [multiply(results[i], norms[i].astype(BF16)) for i in range(2)]
    half = dot(jnp.concatenate(halves(left), axis=1), jnp.concatenate([g, g], axis=0))
    done = product(halves(half), halves(right))
    filled = table_ref[lax.axis_index("own")] >= 0
    out_ref[...] = jnp.where(filled, done, 0.0)


def preconditioned(gt, left, right, table):
    vm = pl.BlockSpec(memory_space=pltpu.VMEM)
    return pl.pallas_call(
        root_kernel,
        name="roots",
        out_shape=jax.ShapeDtypeStruct((R, R), F32),
        in_specs=[vm, vm, vm, pl.BlockSpec(memory_space=pltpu.SMEM)],
        out_specs=vm,
        scratch_shapes=[pltpu.VMEM((2, R, R), F32), pltpu.VMEM((2, R, R), F32)],
        compiler_params=pltpu.CompilerParams(vmem_limit_bytes=16 * 1024 * 1024),
    )(gt, left, right, table)


def shards(
    inputs, cotangent, gate, down_weight, up_weight, mixing, owner_table, left_factor, right_factor
):
    table = owner_table.reshape(-1)
    gt = reduced_block(
        inputs, cotangent, gate.reshape(1, -1), down_weight, up_weight, mixing, table
    )
    return preconditioned(gt, left_factor, right_factor, table)


def solution(mesh):
    in_specs = (
        P(("rep", "own"), None),
        P(("rep", "own"), None),
        P(("rep", "own")),
        P("rep", None),
        P("rep", None),
        P(),
        P(),
        P("own", None, None),
        P("own", None, None),
    )
    return jax.shard_map(
        shards, mesh=mesh, in_specs=in_specs, out_specs=P("own", None), check_vma=False
    )
```

time: 94.6 us -> 85.4 us (0.903)
  Pallas kernels: 94.5 us -> 84.3 us
    pallas_call x1, Pallas kernels: 85.3 us -> 78.4 us  [reduced_block(): pl.pallas_call(reduce_kernel, name='reduce', out_shape=jax.ShapeDtypeStru...]
    pallas_call x1, Pallas kernels: 9.2 us -> 5.92 us  [preconditioned(): pl.pallas_call(root_kernel, name='roots', out_shape=jax.ShapeDtypeStruct(...]
where the time goes in v2:
time: 85.4 us; the launch traced here: 85.3 us
  Pallas kernels  84.3 us (99%)
  local copies, waits for them, and re-layouts  0.91 us (1%)
    pallas_call x1, Pallas kernels, reduced_block(): pl.pallas_call(reduce_kernel, name='reduce', out_shape=jax.ShapeDtypeStru...  78.4 us
    pallas_call x1, Pallas kernels, preconditioned(): pl.pallas_call(root_kernel, name='roots', out_shape=jax.ShapeDtypeStruct(...  5.92 us

profile of v2, /device:TPU:1, one launch (start us, length us, event | category | flops | bytes accessed | tf_op | source)
XLA Modules:
  0.0 85.3 jit_solution(1332523040188153786)
XLA Ops:
  0.0 0.0 copy-start.1
  0.0 0.0 copy-start.2
  0.0 0.0 copy-start.3
  0.0 78.4 %reduce.1.gt_ref = bf16[256,256]{1,0:T(8,128)(2,1)} custom-call(bf16[256,8192]{1,0:T(8,128)(2,1)} %x_hbm.1, bf16[256,8192]{1,0:T(8,128)(2,1)} %cot_hbm.1, f32[1,256]{1,0:T(1,128)} %bitcast.4, bf16[2048,256]{1,0:T(8,128)(2,1)} %down_hbm.1, bf16[2048,256]{1,0:T(8,128)(2,1)} %up_hbm.1, bf16[256,256]{1,0:T(8,128)(2,1)} %mix_ref.1, s32[64]{0:T(128)} %bitcast.2), custom_call_target="tpu_custom_call" | custom-call | tf_op jit(solution)/shard_map/reduce/pallas_call | solution.py:521
  78.4 0.0 copy-done.1
  78.4 0.0 copy-done.2
  78.5 0.0 copy-done.3
  78.5 0.0 copy-start
  78.5 0.9 %copy-done = bf16[256,256]{1,0:T(8,128)(2,1)S(1)} copy-done((bf16[256,256]{1,0:T(8,128)(2,1)S(1)}, bf16[256,256]{1,0:T(8,128)(2,1)}, u32[]{:S(2)}) %copy-start) | copy-done | bytes 131096
  79.4 5.9 %roots.1 = f32[256,256]{1,0:T(8,128)} custom-call(bf16[256,256]{1,0:T(8,128)(2,1)S(1)} %copy-done, f32[1,256,256]{2,1,0:T(8,128)S(1)} %copy-done.1, f32[1,256,256]{2,1,0:T(8,128)S(1)} %copy-done.2, s32[64]{0:T(128)S(1)} %bitcast.3), custom_call_target="tpu_custom_call" | custom-call | tf_op jit(solution)/shard_map/roots/pallas_call | solution.py:639
Async XLA Ops:
  0.0 78.4 %copy-start.1 = (f32[1,256,256]{2,1,0:T(8,128)S(1)}, f32[1,256,256]{2,1,0:T(8,128)}, u32[]{:S(2)}) copy-start(f32[1,256,256]{2,1,0:T(8,128)} %left_ref.1) | copy-start | bytes 786436
  0.0 78.4 %copy-start.2 = (f32[1,256,256]{2,1,0:T(8,128)S(1)}, f32[1,256,256]{2,1,0:T(8,128)}, u32[]{:S(2)}) copy-start(f32[1,256,256]{2,1,0:T(8,128)} %right_ref.1) | copy-start | bytes 786436
  0.0 78.5 %copy-start.3 = (s32[64,1]{0,1:T(1,128)S(1)}, s32[64,1]{0,1:T(1,128)}, u32[]{:S(2)}) copy-start(s32[64,1]{0,1:T(1,128)} %param.15) | copy-start | bytes 772
  78.5 0.9 %copy-start = (bf16[256,256]{1,0:T(8,128)(2,1)S(1)}, bf16[256,256]{1,0:T(8,128)(2,1)}, u32[]{:S(2)}) copy-start(bf16[256,256]{1,0:T(8,128)(2,1)} %reduce.1.gt_ref) | copy-start | bytes 393220

commit v3 on v2

--- a/solution.py
+++ b/solution.py
@@ -23,9 +23,9 @@
 
 
 def reduce_kernel(
-    x_hbm, cot_hbm, gate_ref, down_hbm, up_hbm, mix_ref, table_ref, out_ref,
+    x_hbm, cot_hbm, gate_hbm, down_hbm, up_hbm, mix_hbm, table_hbm, left_hbm, right_hbm, out_ref,
     wbuf, xv, lv, gcol, pacc, sigp, sigr, xp, acc,
-    s1send, s1rel, s1recv, s2f, s2send, s2recv, zf, zsend, zrecv, zag, stage, arecv,
+    s1send, s1rel, s1recv, s2f, s2send, s2recv, zf, zsend, zrecv, zag, stage, arecv, factors, gtv, norms, results, gate_ref, mix_ref, table_ref,
     ld, wsend, w1r, st1r, st2r, zp1, zp2, ddr, xr, gsend, gdr, s1relr, s1r, s2r, zr, zagr, asend, ar,
 ):
     r = lax.axis_index("rep")
@@ -93,6 +93,11 @@
         cols = pl.ds(pl.multiple_of(quarter[s] * 2048, 2048), 2048)
         loads.append(pltpu.make_async_copy(x_hbm.at[:, cols], xv.at[:, cols], ld.at[2 + 2 * s]))
         loads.append(pltpu.make_async_copy(cot_hbm.at[:, cols], lv.at[:, cols], ld.at[3 + 2 * s]))
+    loads.append(pltpu.make_async_copy(left_hbm, factors.at[pl.ds(0, 1)], ld.at[10]))
+    loads.append(pltpu.make_async_copy(right_hbm, factors.at[pl.ds(1, 1)], ld.at[11]))
+    loads.append(pltpu.make_async_copy(gate_hbm, gate_ref, ld.at[12]))
+    loads.append(pltpu.make_async_copy(mix_hbm, mix_ref, ld.at[13]))
+    loads.append(pltpu.make_async_copy(table_hbm, table_ref, ld.at[14]))
     for cp in loads:
         cp.start()
 
@@ -114,7 +119,7 @@
         return wsend.at[nws[0] - 1]
 
     def unit(s, k):
-        return 16 if (s, k) in ((1, 1), (2, 0)) else 32
+        return 32 if s == 3 else 16
 
     def base(s, cc, k):
         return cc * 1024 + (16 * unit(s, 0) if k else 0)
@@ -128,7 +133,9 @@
         return pl.ds(pl.multiple_of(base(s, c, k) + p2 * u, u), u)
 
     def straight(cc, n):
-        return pl.ds(pl.multiple_of(cc * 1024 + 768 + n * 64, 64), 64)
+        size = 128 if n < 3 else 64
+        start = 512 + 128 * min(n, 3) + 64 * max(n - 3, 0)
+        return pl.ds(pl.multiple_of(cc * 1024 + start, 64), size)
 
     def p12(k):
         return (pos[0], pos[1]) if k == 0 else (pos[1], pos[0])
@@ -150,7 +157,7 @@
                 wbuf.at[0, :, rows, :], wbuf.at[s, :, rows, :],
                 wsem(), w1r.at[s - 1, k], zdest[s - 1],
             )
-    for n in range(4):
+    for n in range(5):
         rows = straight(c, n)
         send(wbuf.at[0, :, rows, :], wbuf.at[1, :, rows, :], wsem(), zp1.at[n], zdest[0])
     pair = (r, own_of(x, 1 - zl, y, c))
@@ -205,7 +212,7 @@
         send(wbuf.at[s, :, rows, :], wbuf.at[s, :, rows, :], wsem(), ddr.at[i], partner)
 
     def gathered(cc):
-        return pl.ds(pl.multiple_of(cc * 1024, 256), 768)
+        return pl.ds(pl.multiple_of(cc * 1024, 512), 512)
 
     def d2d(s):
         for k in range(2):
@@ -213,7 +220,7 @@
         to_partner(s, gathered(c), s - 1)
 
     def d2d_straight1():
-        to_partner(1, pl.ds(pl.multiple_of(c * 1024 + 768, 256), 256), 2)
+        to_partner(1, pl.ds(pl.multiple_of(c * 1024 + 512, 512), 512), 2)
 
     def d2d_straight2(n):
         arrived(wbuf.at[2, :, straight(c, n), :], zp2.at[n], pair)
@@ -224,16 +231,16 @@
             if far:
                 stage_far(3, k)
             for i, d in ((3, 2),) if far else ((0, 0), (1, -1), (2, 1)):
-                to_partner(3, rows_at(3, k, 2, d), 7 + k * 4 + i)
+                to_partner(3, rows_at(3, k, 2, d), 8 + k * 4 + i)
 
     def from_partner(s):
         if s < 3:
             arrived(wbuf.at[s, :, gathered(1 - c), :], ddr.at[s - 1], partner)
         if s == 1:
-            rows = pl.ds(pl.multiple_of((1 - c) * 1024 + 768, 256), 256)
+            rows = pl.ds(pl.multiple_of((1 - c) * 1024 + 512, 512), 512)
             arrived(wbuf.at[1, :, rows, :], ddr.at[2], partner)
         if s == 2:
-            for n in range(4):
+            for n in range(5):
                 arrived(wbuf.at[2, :, straight(1 - c, n), :], ddr.at[3 + n], partner)
         if s == 3:
             for k in range(2):
@@ -242,7 +249,7 @@
                     rows = pl.ds(
                         pl.multiple_of(base(3, 1 - c, k) + near(p2, d) * 128, 128), 128
                     )
-                    arrived(wbuf.at[3, :, rows, :], ddr.at[7 + k * 4 + i], partner)
+                    arrived(wbuf.at[3, :, rows, :], ddr.at[8 + k * 4 + i], partner)
         matmul(s, 1 - c)
 
     def cols_of(s):
@@ -275,6 +282,7 @@
 
         lax.fori_loop(0, 2, body, 0)
 
+    loads[12].wait()
     gcol[...] = jnp.transpose(jnp.broadcast_to(gate_ref[...], (128, 256)))
     pacc[...] = jnp.zeros_like(pacc)
     for s in range(4):
@@ -285,38 +293,42 @@
     lift(0, 8, 16)
     s1(3)
     s2(1)
+    s2(2)
     pass_on(0)
-    s2(2)
+    lift(1, 0, 8)
+    s2(3)
     pass_on(1)
-    lift(1, 0, 8)
+    f2(1)
+    lift(1, 8, 16)
     pass_on(2)
-    s2(3)
+    f2(2)
+    matmul(0, c)
     pass_on(3)
-    f2(1)
-    d2d_straight1()
-    lift(1, 8, 16)
-    matmul(0, c)
-    d2d_straight2(0)
-    d2d_straight2(1)
-    f2(2)
-    lift(2, 0, 16)
-    d2d_straight2(2)
-    d2d_straight2(3)
-    matmul(0, 1 - c)
+    lift(2, 0, 8)
     f2(3)
     d2d_last(False)
-    lift(3, 0, 8)
+    d2d_straight2(0)
+    pass_on(4)
+    d2d_straight1()
     d2d(1)
+    lift(2, 8, 16)
+    d2d_straight2(1)
+    d2d(2)
+    lift(3, 0, 16)
+    matmul(0, 1 - c)
     matmul(1, c)
-    lift(3, 8, 16)
-    d2d(2)
-    matmul(2, c)
-    from_partner(1)
+    d2d_straight2(2)
     d2d_last(True)
     matmul(3, c)
+    from_partner(1)
+    d2d_straight2(3)
+    from_partner(3)
+    d2d_straight2(4)
+    matmul(2, c)
     from_partner(2)
-    from_partner(3)
-
+
+    loads[13].wait()
+    loads[14].wait()
     inner = jnp.tanh(pacc[0]).astype(BF16)
     outer = jnp.tanh(jnp.dot(inner, mix_ref[...], preferred_element_type=F32))
     slope = (pacc[1] * (1.0 - outer * outer)).astype(BF16)
@@ -501,19 +513,22 @@
                 tile = arecv[(xx * 4 + yy) * 2 + cc]
                 r0 = cc * 128 + xx * 16 + (yy // 2) * 8
                 l0 = (yy % 2) * 128
-                out_ref[r0 : r0 + 8, l0 : l0 + 128] = tile[0:8]
+                gtv[r0 : r0 + 8, l0 : l0 + 128] = tile[0:8].astype(F32)
                 r1 = cc * 128 + 64 + yy * 16 + (xx // 2) * 8
                 l1 = (xx % 2) * 128
-                out_ref[r1 : r1 + 8, l1 : l1 + 128] = tile[8:16]
+                gtv[r1 : r1 + 8, l1 : l1 + 128] = tile[8:16].astype(F32)
 
     first = pl.ds(0, 31)
     pltpu.make_async_remote_copy(
         src_ref=stage.at[first], dst_ref=arecv.at[first], send_sem=asend, recv_sem=asend,
         device_id=partner, device_id_type=MESH,
     ).wait_send()
-
-
-def reduced_block(inputs, cotangent, gate, down_weight, up_weight, mixing, table):
+    loads[10].wait()
+    loads[11].wait()
+    roots(gtv, factors, norms, results, table_ref[o] >= 0, out_ref)
+
+
+def reduced_block(inputs, cotangent, gate, down_weight, up_weight, mixing, table, left, right):
     any_spec = pl.BlockSpec(memory_space=pltpu.HBM)
     vm = pl.BlockSpec(memory_space=pltpu.VMEM)
     dma = pltpu.SemaphoreType.DMA
@@ -521,9 +536,8 @@
     return pl.pallas_call(
         reduce_kernel,
         name="reduce",
-        out_shape=jax.ShapeDtypeStruct((256, 256), BF16),
-        in_specs=[any_spec, any_spec, vm, any_spec, any_spec, vm,
-                  pl.BlockSpec(memory_space=pltpu.SMEM)],
+        out_shape=jax.ShapeDtypeStruct((256, 256), F32),
+        in_specs=[any_spec] * 9,
         out_specs=vm,
         scratch_shapes=[
             V((4, 2, 2048, 256), BF16),
@@ -547,14 +561,21 @@
             V((32, 16, 128), BF16),
             V((32, 16, 128), BF16),
             V((32, 16, 128), BF16),
-            dma((10,)),
-            dma((94,)),
+            V((2, R, R), F32),
+            V((R, R), F32),
+            V((2, R, R), F32),
+            V((2, R, R), F32),
+            V((1, 256), F32),
+            V((R, R), BF16),
+            pltpu.SMEM((64,), jnp.int32),
+            dma((15,)),
+            dma((97,)),
             dma((3, 2)),
             dma((3, 2, 4)),
             dma((3, 2, 4)),
-            dma((4,)),
-            dma((4,)),
-            dma((15,)),
+            dma((5,)),
+            dma((5,)),
+            dma((16,)),
             dma((4,)),
             dma((54,)),
             dma,
@@ -569,7 +590,7 @@
         compiler_params=pltpu.CompilerParams(
             collective_id=0, has_side_effects=True, vmem_limit_bytes=63 * 1024 * 1024
         ),
-    )(inputs, cotangent, gate, down_weight, up_weight, mixing, table)
+    )(inputs, cotangent, gate, down_weight, up_weight, mixing, table, left, right)
 
 
 def halves(a):
@@ -588,16 +609,16 @@
     return dot(lhs, rhs)
 
 
-def root_kernel(gt_ref, left_ref, right_ref, table_ref, out_ref, norms, results):
+def roots(gt_ref, factors, norms, results, filled, out_ref):
     eye = (
         lax.broadcasted_iota(jnp.int32, (R, R), 0) == lax.broadcasted_iota(jnp.int32, (R, R), 1)
     ).astype(F32)
-    scaled = gt_ref[...].astype(F32) * (1.0 / TOKENS)
+    scaled = gt_ref[...] * (1.0 / TOKENS)
     gt = scaled.astype(BF16)
     g = jnp.transpose(scaled).astype(BF16)
     news = [
-        BETA * left_ref[0] + (1.0 - BETA) * dot(g, gt),
-        BETA * right_ref[0] + (1.0 - BETA) * dot(gt, g),
+        BETA * factors[0] + (1.0 - BETA) * dot(g, gt),
+        BETA * factors[1] + (1.0 - BETA) * dot(gt, g),
     ]
     for i, a in enumerate(news):
         shifted = a + EPS * eye
@@ -630,31 +651,17 @@
     left, right = [multiply(results[i], norms[i].astype(BF16)) for i in range(2)]
     half = dot(jnp.concatenate(halves(left), axis=1), jnp.concatenate([g, g], axis=0))
     done = product(halves(half), halves(right))
-    filled = table_ref[lax.axis_index("own")] >= 0
     out_ref[...] = jnp.where(filled, done, 0.0)
-
-
-def preconditioned(gt, left, right, table):
-    vm = pl.BlockSpec(memory_space=pltpu.VMEM)
-    return pl.pallas_call(
-        root_kernel,
-        name="roots",
-        out_shape=jax.ShapeDtypeStruct((R, R), F32),
-        in_specs=[vm, vm, vm, pl.BlockSpec(memory_space=pltpu.SMEM)],
-        out_specs=vm,
-        scratch_shapes=[pltpu.VMEM((2, R, R), F32), pltpu.VMEM((2, R, R), F32)],
-        compiler_params=pltpu.CompilerParams(vmem_limit_bytes=16 * 1024 * 1024),
-    )(gt, left, right, table)
 
 
 def shards(
     inputs, cotangent, gate, down_weight, up_weight, mixing, owner_table, left_factor, right_factor
 ):
     table = owner_table.reshape(-1)
-    gt = reduced_block(
-        inputs, cotangent, gate.reshape(1, -1), down_weight, up_weight, mixing, table
+    return reduced_block(
+        inputs, cotangent, gate.reshape(1, -1), down_weight, up_weight, mixing, table,
+        left_factor, right_factor,
     )
-    return preconditioned(gt, left_factor, right_factor, table)
 
 
 def solution(mesh):

time: 85.4 us -> 83.1 us (0.973)
  Pallas kernels: 84.3 us -> 81.4 us
    pallas_call x1 -> x0, Pallas kernels: 5.92 us -> none  [preconditioned(): pl.pallas_call(root_kernel, name='roots', out_shape=jax.ShapeDtypeStruct(...]
    pallas_call x1, Pallas kernels: 78.4 us -> 81.4 us  [reduced_block(): pl.pallas_call(reduce_kernel, name='reduce', out_shape=jax.ShapeDtypeStru...]
where the time goes in v3:
time: 83.1 us; the launch traced here: 83 us
  Pallas kernels  81.4 us (98%)
  local copies, waits for them, and re-layouts  1.67 us (2%)
    pallas_call x1, Pallas kernels, reduced_block(): pl.pallas_call(reduce_kernel, name='reduce', out_shape=jax.ShapeDtypeStru...  81.4 us
    unnamed x1, local copies, waits for them, and re-layouts  1.67 us

profile of v3, /device:TPU:1, one launch (start us, length us, event | category | flops | bytes accessed | tf_op | source)
XLA Modules:
  0.0 83.0 jit_solution(16304950873356138718)
XLA Ops:
  0.0 81.4 %reduce.1 = f32[256,256]{1,0:T(8,128)} custom-call(bf16[256,8192]{1,0:T(8,128)(2,1)} %x_hbm.1, bf16[256,8192]{1,0:T(8,128)(2,1)} %cot_hbm.1, f32[1,256]{1,0:T(1,128)} %bitcast.2, bf16[2048,256]{1,0:T(8,128)(2,1)} %down_hbm.1, bf16[2048,256]{1,0:T(8,128)(2,1)} %up_hbm.1, bf16[256,256]{1,0:T(8,128)(2,1)} %mix_hbm.1, s32[64]{0:T(128)} %bitcast.3, ...), custom_call_target="tpu_custom_call" | custom-call | tf_op jit(solution)/shard_map/reduce/pallas_call | solution.py:536
  81.4 1.7 %copy.11 = f32[256,256]{1,0:T(8,128)} copy(f32[256,256]{1,0:T(8,128)} %reduce.1) | data formatting | bytes 524288

commit v4 on v3

--- a/solution.py
+++ b/solution.py
@@ -150,7 +150,7 @@
         (lax.rem(r + sgn + 4, 4), own_of(x, zl, y, c)),
         (lax.rem(r + 2, 4), own_of(x, 1 - zl, y, c)),
     ]
-    for s in (3, 1, 2):
+    for s in (1, 3, 2):
         for k in range(2):
             rows = piece(s, k, *p12(k))
             send(
@@ -236,6 +236,8 @@
     def from_partner(s):
         if s < 3:
             arrived(wbuf.at[s, :, gathered(1 - c), :], ddr.at[s - 1], partner)
+        if s == 2:
+            matmul(2, 1 - c, 0, 1)
         if s == 1:
             rows = pl.ds(pl.multiple_of((1 - c) * 1024 + 512, 512), 512)
             arrived(wbuf.at[1, :, rows, :], ddr.at[2], partner)
@@ -250,7 +252,7 @@
                         pl.multiple_of(base(3, 1 - c, k) + near(p2, d) * 128, 128), 128
                     )
                     arrived(wbuf.at[3, :, rows, :], ddr.at[8 + k * 4 + i], partner)
-        matmul(s, 1 - c)
+        matmul(s, 1 - c, 1 if s == 2 else 0, 2)
 
     def cols_of(s):
         return pl.ds(pl.multiple_of(quarter[s] * 2048, 2048), 2048)
@@ -271,7 +273,7 @@
 
         lax.fori_loop(first, last, body, 0)
 
-    def matmul(s, cc):
+    def matmul(s, cc, first=0, last=2):
         def body(i, carry):
             start = cc * 1024 + i * 512
             rows = pl.ds(pl.multiple_of(start, 512), 512)
@@ -280,7 +282,7 @@
             pacc[1] += jnp.dot(lv[:, cols], wbuf[s, 1, rows, :], preferred_element_type=F32)
             return carry
 
-        lax.fori_loop(0, 2, body, 0)
+        lax.fori_loop(first, last, body, 0)
 
     loads[12].wait()
     gcol[...] = jnp.transpose(jnp.broadcast_to(gate_ref[...], (128, 256)))
@@ -408,7 +410,7 @@
                 ).astype(BF16)
                 return carry
 
-            lax.fori_loop(0, 8, body, 0)
+            lax.fori_loop(0, 8, body, 0, unroll=4)
         near_out(g, 1 + side)
 
     def finish(rnd):
@@ -440,7 +442,7 @@
                     s2send[k, j, rows, :] = part.astype(BF16)
                 return carry
 
-            lax.fori_loop(rnd * 8, rnd * 8 + 8, own_sum, 0)
+            lax.fori_loop(rnd * 8, rnd * 8 + 8, own_sum, 0, unroll=4)
             for d in (2, 1, 3):
                 j = near(pos[1 - k], d)
                 send(
@@ -647,7 +649,7 @@
             norms[i] = advance(m, mb)
         return carry
 
-    lax.fori_loop(0, ITERS - 2, sweep, 0)
+    lax.fori_loop(0, ITERS - 2, sweep, 0, unroll=True)
     left, right = [multiply(results[i], norms[i].astype(BF16)) for i in range(2)]
     half = dot(jnp.concatenate(halves(left), axis=1), jnp.concatenate([g, g], axis=0))
     done = product(halves(half), halves(right))

time: 83.1 us -> 82 us (0.987)
  Pallas kernels: 81.4 us -> 80.3 us
    pallas_call x1, Pallas kernels: 81.4 us -> 80.3 us  [reduced_block(): pl.pallas_call(reduce_kernel, name='reduce', out_shape=jax.ShapeDtypeStru...]
where the time goes in v4:
time: 82 us; the launch traced here: 81.9 us
  Pallas kernels  80.3 us (98%)
  local copies, waits for them, and re-layouts  1.67 us (2%)
    pallas_call x1, Pallas kernels, reduced_block(): pl.pallas_call(reduce_kernel, name='reduce', out_shape=jax.ShapeDtypeStru...  80.3 us
    unnamed x1, local copies, waits for them, and re-layouts  1.67 us

profile of v4, /device:TPU:1, one launch (start us, length us, event | category | flops | bytes accessed | tf_op | source)
XLA Modules:
  0.0 81.9 jit_solution(13329405980140381780)
XLA Ops:
  0.0 80.3 %reduce.1 = f32[256,256]{1,0:T(8,128)} custom-call(bf16[256,8192]{1,0:T(8,128)(2,1)} %x_hbm.1, bf16[256,8192]{1,0:T(8,128)(2,1)} %cot_hbm.1, f32[1,256]{1,0:T(1,128)} %bitcast.2, bf16[2048,256]{1,0:T(8,128)(2,1)} %down_hbm.1, bf16[2048,256]{1,0:T(8,128)(2,1)} %up_hbm.1, bf16[256,256]{1,0:T(8,128)(2,1)} %mix_hbm.1, s32[64]{0:T(128)} %bitcast.3, ...), custom_call_target="tpu_custom_call" | custom-call | tf_op jit(solution)/shard_map/reduce/pallas_call | solution.py:538
  80.3 1.7 %copy.11 = f32[256,256]{1,0:T(8,128)} copy(f32[256,256]{1,0:T(8,128)} %reduce.1) | data formatting | bytes 524288

commit v5 on v4

--- a/solution.py
+++ b/solution.py
@@ -356,7 +356,7 @@
         acc[i] = jnp.dot(sigp[own_rows, :], xv[:, cols], preferred_element_type=F32)
         return carry
 
-    lax.fori_loop(0, 32, own_tokens, 0, unroll=4)
+    lax.fori_loop(0, 32, own_tokens, 0, unroll=8)
     for s in range(4):
         arrived(xp.at[:, cols_of(s)], xr.at[s], partner)
     arrived(sigr, gdr, partner)

time: 82 us -> 81.3 us (level)
  no operation moved by 1% of the time
where the time goes in v5:
time: 81.3 us; the launch traced here: 81.2 us
  Pallas kernels  79.5 us (98%)
  local copies, waits for them, and re-layouts  1.67 us (2%)
    pallas_call x1, Pallas kernels, reduced_block(): pl.pallas_call(reduce_kernel, name='reduce', out_shape=jax.ShapeDtypeStru...  79.5 us
    unnamed x1, local copies, waits for them, and re-layouts  1.67 us

profile of v5, /device:TPU:1, one launch (start us, length us, event | category | flops | bytes accessed | tf_op | source)
XLA Modules:
  0.0 81.2 jit_solution(18202720818811600474)
XLA Ops:
  0.0 79.5 %reduce.1 = f32[256,256]{1,0:T(8,128)} custom-call(bf16[256,8192]{1,0:T(8,128)(2,1)} %x_hbm.1, bf16[256,8192]{1,0:T(8,128)(2,1)} %cot_hbm.1, f32[1,256]{1,0:T(1,128)} %bitcast.2, bf16[2048,256]{1,0:T(8,128)(2,1)} %down_hbm.1, bf16[2048,256]{1,0:T(8,128)(2,1)} %up_hbm.1, bf16[256,256]{1,0:T(8,128)(2,1)} %mix_hbm.1, s32[64]{0:T(128)} %bitcast.3, ...), custom_call_target="tpu_custom_call" | custom-call | tf_op jit(solution)/shard_map/reduce/pallas_call | solution.py:538
  79.5 1.7 %copy.11 = f32[256,256]{1,0:T(8,128)} copy(f32[256,256]{1,0:T(8,128)} %reduce.1) | data formatting | bytes 524288
